TPU v7x, 512 devices: a whole 4x8x8 slice. The times are simulated.
512 devices in a mesh: samp: 64 (over z, y), mark: 8 (over x, core).
Axes of the slice: x: 4, y: 8, z: 8, core: 2. Of those that a mesh axis runs over, the one named last changes fastest.
Arguments:
- dosage: bfloat16 [32768, 2048], P('samp', 'mark'), may hold values from 0 to 2
- alt_count: int32 [2048], P('mark'), may hold values from 40000 to 759999
- obs_count: int32 [2048], P('mark'), may hold values from 400000 to 500000
- sample_weight: float32 [32768], P('samp'), may hold values from 0.25 to 12, as said below
- test_matrix: bfloat16 [2048, 256], P(('mark', 'samp')), may hold values from -6 to 6
Outputs:
- basis: float32 [32768, 256], P(('samp', 'mark'))
- loadings: float32 [2048, 256], P(('mark', 'samp'))
Inputs may be any that keep to these rules, and one draw needn't show every extreme that they name: `sample_weight`: every weight is positive.
All inputs are finite; a program needn't handle non-finite values.
Results may differ from a plain program's by a relative error of at most 0.004.
Values may be sent and summed in bfloat16 or wider, within the bound.
A program may use at most 64 MiB of HBM per device.

v0:
```python
import math

import jax
import jax.numpy as jnp
from jax import lax
from jax.sharding import PartitionSpec as P


def sent_to_all(shard, axis):
    copies = jnp.broadcast_to(shard, (lax.axis_size(axis), *shard.shape))
    return lax.all_to_all(copies, axis, split_axis=0, concat_axis=0, tiled=True)


def laid_out(tiles, dim):
    tiles = jnp.moveaxis(tiles, 0, dim)
    lengths = tiles.shape
    return tiles.reshape(*lengths[:dim], lengths[dim] * lengths[dim + 1], *lengths[dim + 2 :])


def gather_directly(shard, axis, dim):
    tiles = sent_to_all(shard, axis)
    return laid_out(tiles, dim)


def taken_together(shard, axis):
    everything = sent_to_all(shard, axis)
    return jnp.sum(everything, axis=0)


def split_up(shard, dim, length):
    lengths = shard.shape
    tiles = shard.reshape(*lengths[:dim], length, lengths[dim] // length, *lengths[dim + 1 :])
    return jnp.moveaxis(tiles, dim, 0)


def summed_on_arrival(shard, axis, dim):
    tiles = split_up(shard, dim, lax.axis_size(axis))
    arrived = lax.all_to_all(tiles, axis, split_axis=0, concat_axis=0, tiled=True)
    return arrived.sum(axis=0)


def filled_up(lines, length):
    spare = -len(lines) % length
    return jnp.pad(lines, [(0, spare)] + [(0, 0)] * (lines.ndim - 1))


def total_of(shard, axes):
    lines = shard.reshape(-1, shard.shape[-1])
    own = summed_on_arrival(filled_up(lines, lax.axis_size(axes)), axes, 0)
    whole = gather_directly(own, axes, 0)
    return whole[: len(lines)].reshape(shard.shape)


def gram_of(matrix):
    return lax.dot_general(
        matrix,
        matrix,
        (((0,), (0,)), ((), ())),
        precision=lax.Precision.HIGHEST,
        preferred_element_type=jnp.float32,
    )


def per_device(dosage, alt_count, obs_count, sample_weight, test_matrix):
    freq = alt_count.astype(jnp.float32) / (2.0 * obs_count.astype(jnp.float32))
    scale = 1.0 / jnp.sqrt(2.0 * freq * (1.0 - freq))
    standard = (
        jnp.sqrt(sample_weight)[:, None] * (dosage.astype(jnp.float32) - 2.0 * freq) * scale
    ).astype(jnp.bfloat16)
    sample_rows, marker_cols = standard.shape
    rank = test_matrix.shape[1]
    columns = standard
    partial_value = jnp.dot(
        columns, gather_directly(test_matrix, "samp", 0), preferred_element_type=jnp.float32
    )
    share = sample_rows // lax.axis_size("mark")
    sketch = taken_together(partial_value, "mark")
    own_rows = lax.dynamic_slice_in_dim(sketch, lax.axis_index("mark") * share, share, 0)
    gram = gram_of(sketch)
    sketch_round = sketch.astype(jnp.bfloat16)
    lower = jnp.linalg.cholesky(total_of(gram, "samp"))
    inverse = lax.linalg.triangular_solve(
        lower, jnp.eye(rank, dtype=jnp.float32), left_side=True, lower=True
    )
    total_samples = sample_rows * lax.axis_size("samp")
    basis = math.sqrt(total_samples) * jnp.dot(
        own_rows, inverse.T, precision=lax.Precision.HIGHEST, preferred_element_type=jnp.float32
    )
    columns = standard
    projected = summed_on_arrival(
        lax.dot_general(
            columns, sketch_round, (((0,), (0,)), ((), ())), preferred_element_type=jnp.float32
        ),
        "samp",
        0,
    )
    loadings = jnp.dot(
        projected, inverse.T, precision=lax.Precision.HIGHEST, preferred_element_type=jnp.float32
    )
    return (basis, loadings)


def solution(mesh):
    return jax.shard_map(
        per_device,
        mesh=mesh,
        in_specs=(P("samp", "mark"), P("mark"), P("mark"), P("samp"), P(("mark", "samp"), None)),
        out_specs=(P(("samp", "mark"), None), P(("mark", "samp"), None)),
        check_vma=False,
    )
```

profile of v0, /device:TPU:1, one launch (start us, length us, event | category | flops | bytes accessed | tf_op | source)
XLA Modules:
  0.0 208.9 jit_solution(5938978980096521731)
XLA Ops:
  0.6 1.4 broadcast_in_dim.14
  2.0 17.1 %all-to-all-start = ((bf16[64,4,256]{2,1,0:T(4,128)(2,1)}), bf16[64,4,256]{2,1,0:T(4,128)(2,1)S(1)}, u32[]{:S(2)}, u32[]{:S(2)}) async-start(bf16[64,4,256]{2,1,0:T(4,128)(2,1)} %broadcast_in_dim.14), calls=%async_computation | async-start | bytes 262144 | tf_op jit(solution)/shard_map/all_to_all | solution.py:11
  20.5 10.1 %all-to-all-done = bf16[64,4,256]{2,1,0:T(4,128)(2,1)S(1)} async-done(((bf16[64,4,256]{2,1,0:T(4,128)(2,1)}), bf16[64,4,256]{2,1,0:T(4,128)(2,1)S(1)}, u32[]{:S(2)}, u32[]{:S(2)}) %all-to-all-start) | async-done | bytes 131104 | tf_op jit(solution)/shard_map/all_to_all | solution.py:11
  30.7 1.2 fusion.15
  32.3 55.0 %all_to_all.25 = f32[8,512,256]{2,1,0:T(8,128)} all-to-all(f32[8,512,256]{2,1,0:T(8,128)S(1)} %broadcast_in_dim.15), channel_id=1, replica_groups=mesh['samp'=64,'mark'=8] {'mark'}, dimensions={0} | all-to-all | bytes 8388608 | tf_op jit(solution)/shard_map/all_to_all | solution.py:11
  87.3 2.6 %reduce_sum.27 = f32[512,256]{1,0:T(8,128)S(1)} reduce(f32[8,512,256]{2,1,0:T(8,128)} %all_to_all.25, f32[]{:T(128)} %constant.83.clone.1), dimensions={0}, to_apply=%region_0.0 | reduce | flops 917504 | bytes 4718596 | tf_op jit(solution)/shard_map/reduce_sum | solution.py:27
  90.9 0.9 copy.17
  91.7 4.6 %all-to-all-start.2 = ((f32[64,4,256]{2,1,0:T(4,128)}), f32[64,4,256]{2,1,0:T(4,128)S(1)}, u32[]{:S(2)}, u32[]{:S(2)}) async-start(f32[64,4,256]{2,1,0:T(4,128)} %copy.17), calls=%async_computation.2 | async-start | bytes 524288 | tf_op jit(solution)/shard_map/all_to_all | solution.py:38
  96.7 0.8 reshape.37
  97.5 11.5 %all-to-all-done.2 = f32[64,4,256]{2,1,0:T(4,128)S(1)} async-done(((f32[64,4,256]{2,1,0:T(4,128)}), f32[64,4,256]{2,1,0:T(4,128)S(1)}, u32[]{:S(2)}, u32[]{:S(2)}) %all-to-all-start.2) | async-done | bytes 262176 | tf_op jit(solution)/shard_map/all_to_all | solution.py:38
  109.0 5.8 %all-to-all-start.4 = ((f32[64,4,256]{2,1,0:T(4,128)}), f32[64,4,256]{2,1,0:T(4,128)S(1)}, u32[]{:S(2)}, u32[]{:S(2)}) async-start(f32[64,4,256]{2,1,0:T(4,128)} %reshape.37), calls=%async_computation.4 | async-start | bytes 524288 | tf_op jit(solution)/shard_map/all_to_all | solution.py:38
  114.9 12.5 %all-to-all-done.4 = f32[64,4,256]{2,1,0:T(4,128)S(1)} async-done(((f32[64,4,256]{2,1,0:T(4,128)}), f32[64,4,256]{2,1,0:T(4,128)S(1)}, u32[]{:S(2)}, u32[]{:S(2)}) %all-to-all-start.4) | async-done | bytes 262176 | tf_op jit(solution)/shard_map/all_to_all | solution.py:38
  127.4 0.7 broadcast_in_dim.16
  128.1 5.3 %all-to-all-start.3 = ((f32[64,4,256]{2,1,0:T(4,128)}), f32[64,4,256]{2,1,0:T(4,128)S(1)}, u32[]{:S(2)}, u32[]{:S(2)}) async-start(f32[64,4,256]{2,1,0:T(4,128)} %broadcast_in_dim.16), calls=%async_computation.3 | async-start | bytes 524288 | tf_op jit(solution)/shard_map/all_to_all | solution.py:11
  133.6 12.3 %all-to-all-done.3 = f32[64,4,256]{2,1,0:T(4,128)S(1)} async-done(((f32[64,4,256]{2,1,0:T(4,128)}), f32[64,4,256]{2,1,0:T(4,128)S(1)}, u32[]{:S(2)}, u32[]{:S(2)}) %all-to-all-start.3) | async-done | bytes 262176 | tf_op jit(solution)/shard_map/all_to_all | solution.py:11
  146.2 11.7 %cholesky.50 = f32[128,128]{1,0:T(8,128)S(1)} custom-call(f32[128,128]{1,0:T(8,128)S(1)} %cholesky.118), custom_call_target="Cholesky" | custom-call | tf_op jit(solution)/shard_map/jit(cholesky)/cholesky | solution.py:81
  157.9 9.8 %custom-call.14 = f32[1,128,128]{1,2,0:T(8,128)S(1)} custom-call(f32[1,128,128]{2,1,0:T(8,128)S(1)} %get-tuple-element.25), custom_call_target="InvertDiagBlocksLowerTriangular" | custom-call | tf_op jit(solution)/shard_map/jit(cholesky)/cholesky | solution.py:81
  168.2 11.7 %cholesky.105 = f32[128,128]{1,0:T(8,128)S(1)} custom-call(f32[128,128]{1,0:T(8,128)S(1)} %convolution_subtract_fusion.1), custom_call_target="Cholesky" | custom-call | tf_op jit(solution)/shard_map/jit(cholesky)/cholesky | solution.py:81
  182.2 4.1 %while.1 = (s32[]{:T(128)}, f32[256,256]{1,0:T(8,128)S(1)}, s32[2,2]{1,0:T(2,128)S(1)}, f32[2,128,128]{2,1,0:T(8,128)S(1)}, s32[]{:T(128)}) while((s32[]{:T(128)}, f32[256,256]{1,0:T(8,128)S(1)}, s32[2,2]{1,0:T(2,128)S(1)}, f32[2,128,128]{2,1,0:T(8,128)S(1)}, s32[]{:T(128)}) %tuple.28), condition=%wide.while_cond, body=%wide.while_body.sunk | while | flops 2 | bytes 131181 | solution.py:82
  182.8 1.4 bitcast_dynamic-update-slice_fusion.2
  184.8 1.4 bitcast_dynamic-update-slice_fusion.2
  186.3 19.9 %custom-call.15 = f32[2,128,128]{1,2,0:T(8,128)S(1)} custom-call(f32[2,128,128]{2,1,0:T(8,128)S(1)} %get-tuple-element.9), custom_call_target="InvertDiagBlocksLowerTriangular" | custom-call | tf_op jit(solution)/shard_map/triangular_solve | solution.py:82
  207.0 0.9 fusion.6
  207.9 1.0 convolution_multiply_fusion
  (35 shorter events, 7.1 us)
Async XLA Ops:
  2.0 28.7 %all-to-all-start = ((bf16[64,4,256]{2,1,0:T(4,128)(2,1)}), bf16[64,4,256]{2,1,0:T(4,128)(2,1)S(1)}, u32[]{:S(2)}, u32[]{:S(2)}) async-start(bf16[64,4,256]{2,1,0:T(4,128)(2,1)} %broadcast_in_dim.14), calls=%async_computation | async-start | bytes 262144 | tf_op jit(solution)/shard_map/all_to_all | solution.py:11
  87.3 9.1 %copy-start = (bf16[512,256]{1,0:T(8,128)(2,1)S(1)}, bf16[512,256]{1,0:T(8,128)(2,1)}, u32[]{:S(2)}) copy-start(bf16[512,256]{1,0:T(8,128)(2,1)} %param.5) | copy-start | bytes 786436
  91.7 17.3 %all-to-all-start.2 = ((f32[64,4,256]{2,1,0:T(4,128)}), f32[64,4,256]{2,1,0:T(4,128)S(1)}, u32[]{:S(2)}, u32[]{:S(2)}) async-start(f32[64,4,256]{2,1,0:T(4,128)} %copy.17), calls=%async_computation.2 | async-start | bytes 524288 | tf_op jit(solution)/shard_map/all_to_all | solution.py:38
  109.0 18.4 %all-to-all-start.4 = ((f32[64,4,256]{2,1,0:T(4,128)}), f32[64,4,256]{2,1,0:T(4,128)S(1)}, u32[]{:S(2)}, u32[]{:S(2)}) async-start(f32[64,4,256]{2,1,0:T(4,128)} %reshape.37), calls=%async_computation.4 | async-start | bytes 524288 | tf_op jit(solution)/shard_map/all_to_all | solution.py:38
  128.1 17.8 %all-to-all-start.3 = ((f32[64,4,256]{2,1,0:T(4,128)}), f32[64,4,256]{2,1,0:T(4,128)S(1)}, u32[]{:S(2)}, u32[]{:S(2)}) async-start(f32[64,4,256]{2,1,0:T(4,128)} %broadcast_in_dim.16), calls=%async_computation.3 | async-start | bytes 524288 | tf_op jit(solution)/shard_map/all_to_all | solution.py:11
where the time goes:
time: 212 us; the launch traced here: 209 us
  other arithmetic  57.5 us (27%)
  blocking collectives  55 us (26%)
  waiting for transfers between devices  46.4 us (22%)
  starting transfers between devices  32.9 us (16%)
  local copies, waits for them, and re-layouts  9.53 us (4%)
  matrix products  5.5 us (3%)
  between operations  2.19 us (1%)
    all_to_all x1, blocking collectives, sent_to_all(): return lax.all_to_all(copies, axis, split_axis=0, concat_axis=0, tiled=True)  55 us
    another operation x6, other arithmetic, per_device(): lower = jnp.linalg.cholesky(total_of(gram, 'samp'))  34 us
    all_to_all x2, waiting for transfers between devices, summed_on_arrival(): lax.all_to_all(tiles, axis, split_axis=0, concat_axis=0, tiled=True)  24 us
    all_to_all x2, starting transfers between devices, sent_to_all(): return lax.all_to_all(copies, axis, split_axis=0, concat_axis=0, tiled=True)  22.5 us
    all_to_all x2, waiting for transfers between devices, sent_to_all(): return lax.all_to_all(copies, axis, split_axis=0, concat_axis=0, tiled=True)  22.4 us
    another operation x3, other arithmetic, per_device(): lax.linalg.triangular_solve(lower, jnp.eye(rank, dtype=jnp.float32), left...  19.9 us
    all_to_all x2, starting transfers between devices, summed_on_arrival(): lax.all_to_all(tiles, axis, split_axis=0, concat_axis=0, tiled=True)  10.4 us
  transfers between devices with their start and end apart: 4, of which 4 were waited for; matrix products, arithmetic and copies ran while one was open for 1% of the time, Pallas kernels for 0%

commit v1 on v0

v1 whole, which is shorter than its diff:
```python
import functools
import math

import jax
import jax.numpy as jnp
from jax import lax
from jax.experimental import pallas as pl
from jax.experimental.pallas import tpu as pltpu
from jax.sharding import PartitionSpec as P

F32 = jnp.float32
BF16 = jnp.bfloat16
RING = 8
XS = 4
CORES = 2
MARKS = XS * CORES
FAR_RING = (4, 3, 5, 2, 6, 1, 7)
FAR_X = (2, 1, 3)
HIGHEST = lax.Precision.HIGHEST


def inverse_factor(groups):
    lane = lax.broadcasted_iota(jnp.int32, (8, 128), 1)
    row = lax.broadcasted_iota(jnp.int32, (8, 128), 0)
    rows = list(groups)
    count = len(rows)
    for b in range(count):
        start = 8 * b
        inside = (lane >= start) & (lane < start + 8)
        cols = {
            g: [jnp.broadcast_to(rows[g][:, start + j : start + j + 1], (8, 128)) for j in range(8)]
            for g in range(b, count)
        }
        panel = jnp.where(inside, jnp.where(lane - start == row, 1.0, 0.0), rows[b])
        own = cols[b]
        scaled, roots, upper = [], [], {}
        for k in range(8):
            root = lax.rsqrt(jnp.broadcast_to(own[k][k : k + 1], (8, 128)))
            line = jnp.broadcast_to(panel[k : k + 1], (8, 128)) * root
            below = jnp.where(row > k, own[k] * root, 0.0)
            panel = jnp.where(row == k, line, panel - below * line)
            for j in range(k + 1, 8):
                upper[k, j] = jnp.broadcast_to(own[j][k : k + 1], (8, 128)) * root
                own[j] = own[j] - below * upper[k, j]
            scaled.append(line)
            roots.append(root)
        rows[b] = panel
        for g in range(b + 1, count):
            left = jnp.where(inside, 0.0, rows[g])
            theirs = cols[g]
            for k in range(8):
                factor = theirs[k] * roots[k]
                left = left - factor * scaled[k]
                for j in range(k + 1, 8):
                    theirs[j] = theirs[j] - factor * upper[k, j]
            rows[g] = left
    return [jnp.where(lane <= row + 8 * g, rows[g], 0.0) for g in range(count)]


def dot_t(a, b):
    return lax.dot_general(a, b, (((1,), (1,)), ((), ())), precision=HIGHEST, preferred_element_type=F32)


def dot_cols(a, b):
    return lax.dot_general(a, b, (((0,), (0,)), ((), ())), preferred_element_type=F32)


def kernel(
    total,
    dosage_hbm, counts_ref, weight_ref, test_hbm,
    basis_ref, loadings_ref,
    dosage, std, ta, tb, tfull, tbf,
    pair_out, pair_in, sk_out, sk_in, sketch, yr,
    gs, ga, gb, ha, hb, gf, inv,
    pv, pz, ps, py,
    in_sem,
    t1s, t1r, t2s, t2r, prs, prr, sks, skr, yxs, yxr, yps, ypr,
    g1s, g1r, g2s, g2r, fxs, fxr, fps, fpr, z1s, z1r, y1s, y1r,
):
    samp, mark = lax.axis_index("samp"), lax.axis_index("mark")
    z, y = samp // RING, samp % RING
    x, c = mark // CORES, mark % CORES
    partner = (samp, x * CORES + (1 - c))

    def at_y(d):
        return (z * RING + (y + d) % RING, mark)

    def at_z(d):
        return (((z + d) % RING) * RING + y, mark)

    def at_x(d):
        return (samp, ((x + d) % XS) * CORES + c)

    def push(src, dst, send, recv, to):
        copy = pltpu.make_async_remote_copy(
            src_ref=src, dst_ref=dst, send_sem=send, recv_sem=recv,
            device_id=to, device_id_type=pl.DeviceIdType.MESH,
        )
        copy.start()
        return copy

    started = []

    own_a = pltpu.make_async_copy(test_hbm.at[:, pl.ds(0, 128)], ta.at[z, y], in_sem.at[0])
    own_b = pltpu.make_async_copy(test_hbm.at[:, pl.ds(128, 128)], tb.at[y, z], in_sem.at[1])
    own_d = pltpu.make_async_copy(dosage_hbm, dosage, in_sem.at[2])
    own_a.start()
    own_b.start()
    own_d.start()

    barrier = pltpu.get_barrier_semaphore()
    peers = [at_y(d) for d in FAR_RING] + [at_z(d) for d in FAR_RING] + [at_x(d) for d in FAR_X] + [partner]
    for peer in peers:
        pl.semaphore_signal(barrier, inc=1, device_id=peer, device_id_type=pl.DeviceIdType.MESH)
    own_a.wait()
    own_b.wait()
    pl.semaphore_wait(barrier, len(peers))

    first = []
    for d in FAR_RING:
        first.append(push(ta.at[z, y], ta.at[z, y], t1s.at[0, d - 1], t1r.at[0, d - 1], at_y(d)))
        first.append(push(tb.at[y, z], tb.at[y, z], t1s.at[1, d - 1], t1r.at[1, d - 1], at_z(d)))

    own_d.wait()
    alt = counts_ref[0:1].astype(F32)
    obs = counts_ref[1:2].astype(F32)
    freq = alt / (2.0 * obs)
    scale = 1.0 / jnp.sqrt(2.0 * freq * (1.0 - freq))
    roots = jnp.sqrt(weight_ref[...])
    tall = jnp.concatenate([roots] * 2, axis=0).T
    for q in range(4):
        rows = pl.ds(128 * q, 128)
        weights = jnp.broadcast_to(tall[:, q : q + 1], (128, 256))
        std[rows, :] = (weights * (dosage[rows, :].astype(F32) - 2.0 * freq) * scale).astype(BF16)

    for copy in first:
        copy.wait_recv()
    second = []
    for d in FAR_RING:
        second.append(push(ta.at[z], ta.at[z], t2s.at[0, d - 1], t2r.at[0, d - 1], at_z(d)))
        second.append(push(tb.at[y], tb.at[y], t2s.at[1, d - 1], t2r.at[1, d - 1], at_y(d)))
    for copy in second:
        copy.wait_recv()
    started += first + second
    for s in range(RING * RING):
        tfull[4 * s : 4 * s + 4, 0:128] = ta[s // RING, s % RING].astype(F32)
        tfull[4 * s : 4 * s + 4, 128:256] = tb[s % RING, s // RING].astype(F32)
    tbf[...] = tfull[...].astype(BF16)

    def partial_rows(owner):
        rows = pl.ds(pl.multiple_of(owner * 64, 64), 64)
        return jnp.dot(std[rows, :], tbf[...], preferred_element_type=F32)

    pair = {}
    for d in (2, 1, 3, 0):
        pair_out[d] = partial_rows(((x + d) % XS) * CORES + (1 - c))
        pair[d] = push(pair_out.at[d], pair_in.at[d], prs.at[d], prr.at[d], partner)
    mine = {d: partial_rows(((x + d) % XS) * CORES + c) for d in (2, 1, 3, 0)}
    along = {}
    for d in (2, 1, 3):
        pair[d].wait_recv()
        sk_out[d] = mine[d] + pair_in[d]
        along[d] = push(sk_out.at[d], sk_in.at[d], sks.at[d], skr.at[d], at_x(d))
    pair[0].wait_recv()
    own_sketch = mine[0] + pair_in[0]
    for d in (1, 3, 2):
        along[d].wait_recv()
        own_sketch = own_sketch + sk_in[d]
    sketch[...] = own_sketch
    started += list(pair.values()) + list(along.values())

    def gather_over_mark(buf, xs, xr, ps_, pr_):
        out = {d: push(buf.at[mark], buf.at[mark], xs.at[d], xr.at[d], at_x(d)) for d in FAR_X}
        over = {0: push(buf.at[mark], buf.at[mark], ps_.at[0], pr_.at[0], partner)}
        for d in (1, 3, 2):
            out[d].wait_recv()
            slot = ((x + XS - d) % XS) * CORES + c
            over[d] = push(buf.at[slot], buf.at[slot], ps_.at[d], pr_.at[d], partner)
        for d in (0, 1, 3, 2):
            over[d].wait_recv()
        started.extend(list(out.values()) + list(over.values()))

    yr[mark] = own_sketch.astype(BF16)
    gather_over_mark(yr, yxs, yxr, yps, ypr)
    rounded = yr[...].reshape(512, 256)

    left = dot_cols(rounded, rounded[:, 0:128])
    gs[0:256, :] = left
    gs[256:384, :] = dot_cols(rounded[:, 128:256], rounded[:, 128:256])
    part = pl.multiple_of(mark * 48, 8)
    ga[y] = gs[pl.ds(part, 24), :]
    gb[z] = gs[pl.ds(pl.multiple_of(part + 24, 8), 24), :]
    first = []
    for d in FAR_RING:
        first.append(push(ga.at[y], ga.at[y], g1s.at[0, d - 1], g1r.at[0, d - 1], at_y(d)))
        first.append(push(gb.at[z], gb.at[z], g1s.at[1, d - 1], g1r.at[1, d - 1], at_z(d)))

    pv[...] = dot_cols(std[...], rounded).reshape(RING, 32, 256)

    for copy in first:
        copy.wait_recv()
    ha[z] = jnp.sum(ga[...], axis=0)
    hb[y] = jnp.sum(gb[...], axis=0)
    second = []
    for d in FAR_RING:
        second.append(push(ha.at[z], ha.at[z], g2s.at[0, d - 1], g2r.at[0, d - 1], at_z(d)))
        second.append(push(hb.at[y], hb.at[y], g2s.at[1, d - 1], g2r.at[1, d - 1], at_y(d)))
    zsum = {}
    for d in FAR_RING:
        zsum[d] = push(pv.at[(z + d) % RING], pz.at[d], z1s.at[d], z1r.at[d], at_z(d))
    for copy in second:
        copy.wait_recv()
    started += first + second
    gf[mark] = jnp.concatenate([jnp.sum(ha[...], axis=0), jnp.sum(hb[...], axis=0)], axis=0)
    gather_over_mark(gf, fxs, fxr, fps, fpr)
    gs[...] = gf[...].reshape(384, 128)

    one = inverse_factor([gs[8 * g : 8 * g + 8, :] for g in range(16)])
    for g in range(16):
        inv[0, 8 * g : 8 * g + 8, :] = one[g]
    inv1 = inv[0]
    low = dot_t(gs[128:256, :], inv1)
    gs[256:384, :] = gs[256:384, :] - dot_t(low, low)

    psum = pv[z]
    for d in range(1, RING):
        zsum[d].wait_recv()
        psum = psum + pz[d]
    for q in range(RING):
        ps[q] = psum[4 * q : 4 * q + 4, :]
    ysum = {d: push(ps.at[(y + d) % RING], py.at[d], y1s.at[d], y1r.at[d], at_y(d)) for d in FAR_RING}
    started += list(zsum.values()) + list(ysum.values())

    two = inverse_factor([gs[256 + 8 * g : 264 + 8 * g, :] for g in range(16)])
    for g in range(16):
        inv[1, 8 * g : 8 * g + 8, :] = two[g]
    inv2 = inv[1]

    own_sketch = sketch[...]
    head = dot_t(own_sketch[:, 0:128], inv1)
    tail = dot_t(own_sketch[:, 128:256] - dot_t(head, low), inv2)
    basis_ref[:, 0:128] = math.sqrt(total) * head
    basis_ref[:, 128:256] = math.sqrt(total) * tail

    projected = ps[y]
    for d in range(1, RING):
        ysum[d].wait_recv()
        projected = projected + py[d]
    projected = jnp.concatenate([projected, projected], axis=0)
    head = dot_t(projected[:, 0:128], inv1)
    tail = dot_t(projected[:, 128:256] - dot_t(head, low), inv2)
    loadings_ref[:, 0:128] = head[0:4]
    loadings_ref[:, 128:256] = tail[0:4]

    for copy in started:
        copy.wait_send()


def per_device(dosage, alt_count, obs_count, sample_weight, test_matrix):
    counts = jnp.stack([alt_count, obs_count])
    weights = sample_weight.reshape(4, 128)
    total = dosage.shape[0] * lax.axis_size("samp")
    dma = pltpu.SemaphoreType.DMA
    vmem = pl.BlockSpec(memory_space=pltpu.VMEM)
    hbm = pl.BlockSpec(memory_space=pl.ANY)
    two_rings = [dma((2, RING - 1))] * 2
    return pl.pallas_call(
        functools.partial(kernel, total),
        out_shape=(
            jax.ShapeDtypeStruct((64, 256), F32),
            jax.ShapeDtypeStruct((4, 256), F32),
        ),
        in_specs=[hbm, vmem, vmem, hbm],
        out_specs=(vmem, vmem),
        scratch_shapes=[
            pltpu.VMEM((512, 256), BF16),
            pltpu.VMEM((512, 256), BF16),
            pltpu.VMEM((RING, RING, 4, 128), BF16),
            pltpu.VMEM((RING, RING, 4, 128), BF16),
            pltpu.VMEM((256, 256), F32),
            pltpu.VMEM((256, 256), BF16),
            pltpu.VMEM((XS, 64, 256), F32),
            pltpu.VMEM((XS, 64, 256), F32),
            pltpu.VMEM((XS, 64, 256), F32),
            pltpu.VMEM((XS, 64, 256), F32),
            pltpu.VMEM((64, 256), F32),
            pltpu.VMEM((MARKS, 64, 256), BF16),
            pltpu.VMEM((384, 128), F32),
            pltpu.VMEM((RING, 24, 128), F32),
            pltpu.VMEM((RING, 24, 128), F32),
            pltpu.VMEM((RING, 24, 128), F32),
            pltpu.VMEM((RING, 24, 128), F32),
            pltpu.VMEM((MARKS, 48, 128), F32),
            pltpu.VMEM((2, 128, 128), F32),
            pltpu.VMEM((RING, 32, 256), F32),
            pltpu.VMEM((RING, 32, 256), F32),
            pltpu.VMEM((RING, 4, 256), F32),
            pltpu.VMEM((RING, 4, 256), F32),
            dma((3,)),
            *two_rings, *two_rings,
            *[dma((XS,))] * 8,
            *two_rings, *two_rings,
            *[dma((XS,))] * 4,
            *[dma((RING,))] * 4,
        ],
        compiler_params=pltpu.CompilerParams(collective_id=0, has_side_effects=True),
    )(dosage, counts, weights, test_matrix)


def solution(mesh):
    return jax.shard_map(
        per_device,
        mesh=mesh,
        in_specs=(P("samp", "mark"), P("mark"), P("mark"), P("samp"), P(("mark", "samp"), None)),
        out_specs=(P(("samp", "mark"), None), P(("mark", "samp"), None)),
        check_vma=False,
    )
```

time: 212 us -> 69.8 us (0.33); the launches traced: 209 us -> 69.6 us
  Pallas kernels: 0 us -> 65.6 us
  other arithmetic: 57.5 us -> 0.58 us
  blocking collectives: 55 us -> 0 us
  waiting for transfers between devices: 46.4 us -> 0 us
  starting transfers between devices: 32.9 us -> 0 us
  local copies, waits for them, and re-layouts: 9.53 us -> 2.75 us
  matrix products: 5.5 us -> 0 us
    pallas_call x0 -> x1, Pallas kernels: none -> 65.6 us  [per_device(): pl.pallas_call(functools.partial(kernel, total), out_shape=(jax.ShapeDtyp...]
    all_to_all x1 -> x0, blocking collectives: 55 us -> none  [sent_to_all(): return lax.all_to_all(copies, axis, split_axis=0, concat_axis=0, tiled=True)]
    another operation x9 -> x1, other arithmetic: 54 us -> 0.58 us  [per_device(): counts = jnp.stack([alt_count, obs_count])]
    all_to_all x4 -> x0, waiting for transfers between devices: 46.4 us -> none  [the longest x2 24 us: summed_on_arrival(): lax.all_to_all(tiles, axis, split_axis=0, concat_axis=0, tiled=True)]
    all_to_all x4 -> x0, starting transfers between devices: 32.9 us -> none  [the longest x2 22.5 us: sent_to_all(): return lax.all_to_all(copies, axis, split_axis=0, concat_axis=0, tiled=True)]
    dot_general x5 -> x0, matrix products: 4.19 us -> none  [the longest x1 1.22 us: per_device(): jnp.dot(columns, gather_directly(test_matrix, 'samp', 0), preferred_eleme...]
    another operation x9 -> x0, local copies, waits for them, and re-layouts: 4.16 us -> none
    unnamed x2 -> x8, local copies, waits for them, and re-layouts: 0.01 us -> 2.75 us
  transfers between devices with their start and end apart: 4 -> 0, of which waited for: 4 -> 0; matrix products, arithmetic and copies ran while one was open for 1% -> 0% of each run, Pallas kernels for 0% -> 0%
where the time goes in v1:
time: 69.8 us; the launch traced here: 69.6 us
  Pallas kernels  65.6 us (94%)
  local copies, waits for them, and re-layouts  2.75 us (4%)
    pallas_call x1, Pallas kernels, per_device(): pl.pallas_call(functools.partial(kernel, total), out_shape=(jax.ShapeDtyp...  65.6 us
    unnamed x8, local copies, waits for them, and re-layouts  2.75 us

profile of v1, /device:TPU:1, one launch (start us, length us, event | category | flops | bytes accessed | tf_op | source)
XLA Modules:
  0.0 69.6 jit_solution(17123795832616358968)
XLA Ops:
  0.6 0.0 copy-start.2
  0.6 0.0 copy-start.1
  0.6 0.7 copy-done.2
  1.3 0.0 copy-done.1
  1.3 0.6 pad_add_fusion.counts_ref
  1.9 65.6 %shard_map.68 = (f32[64,256]{1,0:T(8,128)}, f32[4,256]{1,0:T(4,128)}) custom-call(bf16[512,256]{1,0:T(8,128)(2,1)} %dosage_hbm.1, s32[2,256]{1,0:T(2,128)} %pad_add_fusion.counts_ref, f32[4,128]{1,0:T(4,128)} %bitcast.3, bf16[4,256]{1,0:T(4,128)(2,1)} %test_hbm.1), custom_call_target="tpu_custom_call" | custom-call | tf_op jit(solution)/shard_map/pallas_call | solution.py:267
  67.5 0.0 copy-start
  67.5 1.5 %copy.9 = f32[64,256]{1,0:T(8,128)} copy(f32[64,256]{1,0:T(8,128)} %get-tuple-element.4) | data formatting | bytes 131072
  69.0 0.0 copy-done
  69.0 0.6 copy.10
Async XLA Ops:
  0.6 0.7 copy-start.2
  0.6 0.7 copy-start.1
  67.5 1.5 %copy-start = (f32[4,256]{1,0:T(4,128)S(1)}, f32[4,256]{1,0:T(4,128)}, u32[]{:S(2)}) copy-start(f32[4,256]{1,0:T(4,128)} %get-tuple-element.5) | copy-start | bytes 12292

commit v2 on v1

--- a/solution.py
+++ b/solution.py
@@ -19,41 +19,56 @@
 HIGHEST = lax.Precision.HIGHEST
 
 
+def spread(column):
+    return jnp.broadcast_to(column, (8, 128))
+
+
 def inverse_factor(groups):
     lane = lax.broadcasted_iota(jnp.int32, (8, 128), 1)
     row = lax.broadcasted_iota(jnp.int32, (8, 128), 0)
     rows = list(groups)
     count = len(rows)
+    own = [spread(rows[0][:, j : j + 1]) for j in range(8)]
     for b in range(count):
         start = 8 * b
         inside = (lane >= start) & (lane < start + 8)
-        cols = {
-            g: [jnp.broadcast_to(rows[g][:, start + j : start + j + 1], (8, 128)) for j in range(8)]
-            for g in range(b, count)
-        }
+        cols = {g: [spread(rows[g][:, start + j : start + j + 1]) for j in range(8)] for g in range(b + 1, count)}
+        last = b + 1 == count
+        following = None if last else [spread(rows[b + 1][:, start + 8 + j : start + 9 + j]) for j in range(8)]
         panel = jnp.where(inside, jnp.where(lane - start == row, 1.0, 0.0), rows[b])
-        own = cols[b]
-        scaled, roots, upper = [], [], {}
+        scaled, roots, upper, near = [], [], {}, []
         for k in range(8):
-            root = lax.rsqrt(jnp.broadcast_to(own[k][k : k + 1], (8, 128)))
-            line = jnp.broadcast_to(panel[k : k + 1], (8, 128)) * root
-            below = jnp.where(row > k, own[k] * root, 0.0)
-            panel = jnp.where(row == k, line, panel - below * line)
+            root = lax.rsqrt(spread(own[k][k : k + 1]))
+            line = spread(panel[k : k + 1]) * root
+            below = own[k] * root
             for j in range(k + 1, 8):
-                upper[k, j] = jnp.broadcast_to(own[j][k : k + 1], (8, 128)) * root
+                upper[k, j] = spread(own[j][k : k + 1]) * root
                 own[j] = own[j] - below * upper[k, j]
+            panel = jnp.where(row == k, line, panel - jnp.where(row > k, below, 0.0) * line)
             scaled.append(line)
             roots.append(root)
+            if not last:
+                theirs = cols[b + 1]
+                factor = theirs[k] * root
+                for j in range(k + 1, 8):
+                    theirs[j] = theirs[j] - factor * upper[k, j]
+                for j in range(8):
+                    following[j] = following[j] - factor * spread(factor[j : j + 1])
+                near.append(factor)
         rows[b] = panel
         for g in range(b + 1, count):
             left = jnp.where(inside, 0.0, rows[g])
             theirs = cols[g]
             for k in range(8):
-                factor = theirs[k] * roots[k]
+                if g == b + 1:
+                    factor = near[k]
+                else:
+                    factor = theirs[k] * roots[k]
+                    for j in range(k + 1, 8):
+                        theirs[j] = theirs[j] - factor * upper[k, j]
                 left = left - factor * scaled[k]
-                for j in range(k + 1, 8):
-                    theirs[j] = theirs[j] - factor * upper[k, j]
             rows[g] = left
+        own = following
     return [jnp.where(lane <= row + 8 * g, rows[g], 0.0) for g in range(count)]
 
 
@@ -67,9 +82,9 @@
 
 def kernel(
     total,
-    dosage_hbm, counts_ref, weight_ref, test_hbm,
+    dosage_hbm, alt_hbm, obs_hbm, weight_hbm, test_hbm,
     basis_ref, loadings_ref,
-    dosage, std, ta, tb, tfull, tbf,
+    dosage, alt, obs, weight, std, ta, tb, tfull, tbf,
     pair_out, pair_in, sk_out, sk_in, sketch, yr,
     gs, ga, gb, ha, hb, gf, inv,
     pv, pz, ps, py,
@@ -103,10 +118,16 @@
 
     own_a = pltpu.make_async_copy(test_hbm.at[:, pl.ds(0, 128)], ta.at[z, y], in_sem.at[0])
     own_b = pltpu.make_async_copy(test_hbm.at[:, pl.ds(128, 128)], tb.at[y, z], in_sem.at[1])
-    own_d = pltpu.make_async_copy(dosage_hbm, dosage, in_sem.at[2])
+    rest = [
+        pltpu.make_async_copy(src, dst, in_sem.at[2 + i])
+        for i, (src, dst) in enumerate(
+            ((dosage_hbm, dosage), (alt_hbm, alt), (obs_hbm, obs), (weight_hbm, weight))
+        )
+    ]
     own_a.start()
     own_b.start()
-    own_d.start()
+    for copy in rest:
+        copy.start()
 
     barrier = pltpu.get_barrier_semaphore()
     peers = [at_y(d) for d in FAR_RING] + [at_z(d) for d in FAR_RING] + [at_x(d) for d in FAR_X] + [partner]
@@ -121,17 +142,19 @@
         first.append(push(ta.at[z, y], ta.at[z, y], t1s.at[0, d - 1], t1r.at[0, d - 1], at_y(d)))
         first.append(push(tb.at[y, z], tb.at[y, z], t1s.at[1, d - 1], t1r.at[1, d - 1], at_z(d)))
 
-    own_d.wait()
-    alt = counts_ref[0:1].astype(F32)
-    obs = counts_ref[1:2].astype(F32)
-    freq = alt / (2.0 * obs)
+    for copy in rest:
+        copy.wait()
+    freq = alt[...].astype(F32) / (2.0 * obs[...].astype(F32))
     scale = 1.0 / jnp.sqrt(2.0 * freq * (1.0 - freq))
-    roots = jnp.sqrt(weight_ref[...])
+    roots = jnp.sqrt(weight[...])
     tall = jnp.concatenate([roots] * 2, axis=0).T
     for q in range(4):
         rows = pl.ds(128 * q, 128)
-        weights = jnp.broadcast_to(tall[:, q : q + 1], (128, 256))
-        std[rows, :] = (weights * (dosage[rows, :].astype(F32) - 2.0 * freq) * scale).astype(BF16)
+        weights = jnp.broadcast_to(tall[:, q : q + 1], (128, 128))
+        for h in range(2):
+            cols = pl.ds(128 * h, 128)
+            centred = dosage[rows, cols].astype(F32) - 2.0 * freq[h : h + 1]
+            std[rows, cols] = (weights * centred * scale[h : h + 1]).astype(BF16)
 
     for copy in first:
         copy.wait_recv()
@@ -215,13 +238,6 @@
     gather_over_mark(gf, fxs, fxr, fps, fpr)
     gs[...] = gf[...].reshape(384, 128)
 
-    one = inverse_factor([gs[8 * g : 8 * g + 8, :] for g in range(16)])
-    for g in range(16):
-        inv[0, 8 * g : 8 * g + 8, :] = one[g]
-    inv1 = inv[0]
-    low = dot_t(gs[128:256, :], inv1)
-    gs[256:384, :] = gs[256:384, :] - dot_t(low, low)
-
     psum = pv[z]
     for d in range(1, RING):
         zsum[d].wait_recv()
@@ -231,49 +247,72 @@
     ysum = {d: push(ps.at[(y + d) % RING], py.at[d], y1s.at[d], y1r.at[d], at_y(d)) for d in FAR_RING}
     started += list(zsum.values()) + list(ysum.values())
 
+    one = inverse_factor([gs[8 * g : 8 * g + 8, :] for g in range(16)])
+    for g in range(16):
+        inv[0, 8 * g : 8 * g + 8, :] = one[g]
+    inv1 = inv[0]
+    low = dot_t(gs[128:256, :], inv1)
+    gs[256:384, :] = gs[256:384, :] - dot_t(low, low)
+
+    head = dot_t(sketch[:, 0:128], inv1)
+    middle = sketch[:, 128:256] - dot_t(head, low)
+
     two = inverse_factor([gs[256 + 8 * g : 264 + 8 * g, :] for g in range(16)])
     for g in range(16):
         inv[1, 8 * g : 8 * g + 8, :] = two[g]
     inv2 = inv[1]
-
-    own_sketch = sketch[...]
-    head = dot_t(own_sketch[:, 0:128], inv1)
-    tail = dot_t(own_sketch[:, 128:256] - dot_t(head, low), inv2)
-    basis_ref[:, 0:128] = math.sqrt(total) * head
-    basis_ref[:, 128:256] = math.sqrt(total) * tail
-
     projected = ps[y]
     for d in range(1, RING):
         ysum[d].wait_recv()
         projected = projected + py[d]
     projected = jnp.concatenate([projected, projected], axis=0)
-    head = dot_t(projected[:, 0:128], inv1)
-    tail = dot_t(projected[:, 128:256] - dot_t(head, low), inv2)
-    loadings_ref[:, 0:128] = head[0:4]
-    loadings_ref[:, 128:256] = tail[0:4]
+    head_p = dot_t(projected[:, 0:128], inv1)
+    middle_p = projected[:, 128:256] - dot_t(head_p, low)
+    tail = dot_t(jnp.concatenate([middle, middle_p], axis=0), inv2)
+    basis_ref[:, 0:128] = math.sqrt(total) * head
+    basis_ref[:, 128:256] = math.sqrt(total) * tail[0:64]
+    loadings_ref[:, 0:128] = head_p[0:4]
+    loadings_ref[:, 128:256] = tail[64:68]
 
     for copy in started:
         copy.wait_send()
 
 
+def hand_over(basis_in, loadings_in, basis_out, loadings_out, sems):
+    copies = [
+        pltpu.make_async_copy(basis_in, basis_out, sems.at[0]),
+        pltpu.make_async_copy(loadings_in, loadings_out, sems.at[1]),
+    ]
+    for copy in copies:
+        copy.start()
+    for copy in copies:
+        copy.wait()
+
+
 def per_device(dosage, alt_count, obs_count, sample_weight, test_matrix):
-    counts = jnp.stack([alt_count, obs_count])
-    weights = sample_weight.reshape(4, 128)
     total = dosage.shape[0] * lax.axis_size("samp")
     dma = pltpu.SemaphoreType.DMA
     vmem = pl.BlockSpec(memory_space=pltpu.VMEM)
-    hbm = pl.BlockSpec(memory_space=pl.ANY)
+    hbm = pl.BlockSpec(memory_space=pltpu.HBM)
     two_rings = [dma((2, RING - 1))] * 2
-    return pl.pallas_call(
+    shapes = ((64, 256), F32), ((4, 256), F32)
+    args = (
+        dosage,
+        alt_count.reshape(2, 128),
+        obs_count.reshape(2, 128),
+        sample_weight.reshape(4, 128),
+        test_matrix,
+    )
+    basis, loadings = pl.pallas_call(
         functools.partial(kernel, total),
-        out_shape=(
-            jax.ShapeDtypeStruct((64, 256), F32),
-            jax.ShapeDtypeStruct((4, 256), F32),
-        ),
-        in_specs=[hbm, vmem, vmem, hbm],
+        out_shape=tuple(pltpu.VMEM(*s) for s in shapes),
+        in_specs=[hbm] * 5,
         out_specs=(vmem, vmem),
         scratch_shapes=[
             pltpu.VMEM((512, 256), BF16),
+            pltpu.VMEM((2, 128), jnp.int32),
+            pltpu.VMEM((2, 128), jnp.int32),
+            pltpu.VMEM((4, 128), F32),
             pltpu.VMEM((512, 256), BF16),
             pltpu.VMEM((RING, RING, 4, 128), BF16),
             pltpu.VMEM((RING, RING, 4, 128), BF16),
@@ -296,15 +335,25 @@
             pltpu.VMEM((RING, 32, 256), F32),
             pltpu.VMEM((RING, 4, 256), F32),
             pltpu.VMEM((RING, 4, 256), F32),
-            dma((3,)),
+            dma((6,)),
             *two_rings, *two_rings,
             *[dma((XS,))] * 8,
             *two_rings, *two_rings,
             *[dma((XS,))] * 4,
             *[dma((RING,))] * 4,
         ],
-        compiler_params=pltpu.CompilerParams(collective_id=0, has_side_effects=True),
-    )(dosage, counts, weights, test_matrix)
+        compiler_params=pltpu.CompilerParams(
+            collective_id=0, has_side_effects=True, vmem_limit_bytes=24 * 1024 * 1024
+        ),
+    )(*[pltpu.with_memory_space_constraint(arg, pltpu.HBM) for arg in args])
+    return pl.pallas_call(
+        hand_over,
+        out_shape=tuple(jax.ShapeDtypeStruct(*s) for s in shapes),
+        in_specs=[vmem] * 2,
+        out_specs=(hbm, hbm),
+        scratch_shapes=[dma((2,))],
+        compiler_params=pltpu.CompilerParams(vmem_limit_bytes=1024 * 1024),
+    )(basis, loadings)
 
 
 def solution(mesh):

time: 69.8 us -> 62.8 us (0.90)
  Pallas kernels: 65.6 us -> 62 us
  local copies, waits for them, and re-layouts: 2.75 us -> 0 us
    pallas_call x1 -> x2, Pallas kernels: 65.6 us -> 62 us  [the longest x1 61.4 us: per_device(): pl.pallas_call(functools.partial(kernel, total), out_shape=tuple((pltpu.V...]
    unnamed x8 -> x0, local copies, waits for them, and re-layouts: 2.75 us -> none
where the time goes in v2:
time: 62.8 us; the launch traced here: 62.6 us
  Pallas kernels  62 us (99%)
  between operations  0.64 us (1%)
    pallas_call x1, Pallas kernels, per_device(): pl.pallas_call(functools.partial(kernel, total), out_shape=tuple((pltpu.V...  61.4 us

profile of v2, /device:TPU:1, one launch (start us, length us, event | category | flops | bytes accessed | tf_op | source)
XLA Modules:
  0.0 62.6 jit_solution(16949219389308173671)
XLA Ops:
  0.6 61.4 %shard_map.68 = (f32[64,256]{1,0:T(8,128)S(1)}, f32[4,256]{1,0:T(4,128)S(1)}) custom-call(bf16[512,256]{1,0:T(8,128)(2,1)} %dosage_hbm.1, s32[2,128]{1,0:T(2,128)} %bitcast.4, s32[2,128]{1,0:T(2,128)} %bitcast.5, f32[4,128]{1,0:T(4,128)} %bitcast.3, bf16[4,256]{1,0:T(4,128)(2,1)} %test_hbm.1), custom_call_target="tpu_custom_call" | custom-call | tf_op jit(solution)/shard_map/pallas_call | solution.py:306
  62.0 0.7 %shard_map.69 = (f32[64,256]{1,0:T(8,128)}, f32[4,256]{1,0:T(4,128)}) custom-call(f32[64,256]{1,0:T(8,128)S(1)} %get-tuple-element.4.basis_in, f32[4,256]{1,0:T(4,128)S(1)} %get-tuple-element.5.loadings_in), custom_call_target="tpu_custom_call" | custom-call | tf_op jit(solution)/shard_map/pallas_call | solution.py:349

commit v3 on v2

--- a/solution.py
+++ b/solution.py
@@ -23,13 +23,15 @@
     return jnp.broadcast_to(column, (8, 128))
 
 
-def inverse_factor(groups):
+def inverse_factor(groups, meanwhile=None):
     lane = lax.broadcasted_iota(jnp.int32, (8, 128), 1)
     row = lax.broadcasted_iota(jnp.int32, (8, 128), 0)
     rows = list(groups)
     count = len(rows)
     own = [spread(rows[0][:, j : j + 1]) for j in range(8)]
     for b in range(count):
+        if meanwhile is not None and b in meanwhile:
+            meanwhile[b]()
         start = 8 * b
         inside = (lane >= start) & (lane < start + 8)
         cols = {g: [spread(rows[g][:, start + j : start + j + 1]) for j in range(8)] for g in range(b + 1, count)}
@@ -85,12 +87,13 @@
     dosage_hbm, alt_hbm, obs_hbm, weight_hbm, test_hbm,
     basis_ref, loadings_ref,
     dosage, alt, obs, weight, std, ta, tb, tfull, tbf,
-    pair_out, pair_in, sk_out, sk_in, sketch, yr,
-    gs, ga, gb, ha, hb, gf, inv,
-    pv, pz, ps, py,
+    partial, pair_in, sk_out, sk_in, sketch, yr0, yr1,
+    g1, g2, ga1, gb1, ha1, hb1, gf1, ga2, gb2, ha2, hb2, gf2, inv,
+    pva, pvb, pza, pzb, psa, psb, pya, pyb, pm,
     in_sem,
-    t1s, t1r, t2s, t2r, prs, prr, sks, skr, yxs, yxr, yps, ypr,
-    g1s, g1r, g2s, g2r, fxs, fxr, fps, fpr, z1s, z1r, y1s, y1r,
+    t1s, t1r, t2s, t2r, prs, prr, sks, skr, yxs, yxr, yps, ypr, y2s, y2r,
+    g11s, g11r, g12s, g12r, g21s, g21r, g22s, g22r,
+    fxs, fxr, f2s, f2r, z1s, z1r, y1s, y1r,
 ):
     samp, mark = lax.axis_index("samp"), lax.axis_index("mark")
     z, y = samp // RING, samp % RING
@@ -105,6 +108,9 @@
 
     def at_x(d):
         return (samp, ((x + d) % XS) * CORES + c)
+
+    def at_other(d):
+        return (samp, ((x + d) % XS) * CORES + (1 - c))
 
     def push(src, dst, send, recv, to):
         copy = pltpu.make_async_remote_copy(
@@ -130,7 +136,8 @@
         copy.start()
 
     barrier = pltpu.get_barrier_semaphore()
-    peers = [at_y(d) for d in FAR_RING] + [at_z(d) for d in FAR_RING] + [at_x(d) for d in FAR_X] + [partner]
+    peers = [at_y(d) for d in FAR_RING] + [at_z(d) for d in FAR_RING] + [at_x(d) for d in FAR_X]
+    peers += [at_other(d) for d in FAR_X] + [partner]
     for peer in peers:
         pl.semaphore_signal(barrier, inc=1, device_id=peer, device_id_type=pl.DeviceIdType.MESH)
     own_a.wait()
@@ -170,108 +177,160 @@
         tfull[4 * s : 4 * s + 4, 128:256] = tb[s % RING, s // RING].astype(F32)
     tbf[...] = tfull[...].astype(BF16)
 
-    def partial_rows(owner):
-        rows = pl.ds(pl.multiple_of(owner * 64, 64), 64)
-        return jnp.dot(std[rows, :], tbf[...], preferred_element_type=F32)
-
-    pair = {}
-    for d in (2, 1, 3, 0):
-        pair_out[d] = partial_rows(((x + d) % XS) * CORES + (1 - c))
-        pair[d] = push(pair_out.at[d], pair_in.at[d], prs.at[d], prr.at[d], partner)
-    mine = {d: partial_rows(((x + d) % XS) * CORES + c) for d in (2, 1, 3, 0)}
-    along = {}
-    for d in (2, 1, 3):
-        pair[d].wait_recv()
-        sk_out[d] = mine[d] + pair_in[d]
-        along[d] = push(sk_out.at[d], sk_in.at[d], sks.at[d], skr.at[d], at_x(d))
-    pair[0].wait_recv()
-    own_sketch = mine[0] + pair_in[0]
+    def block(d, core):
+        return ((x + d) % XS) * CORES + core
+
+    steps = [(h, d) for h in range(2) for d in (2, 1, 3, 0)]
+    pair, along = {}, {}
+    for h, d in steps:
+        if d == 2:
+            half = jnp.dot(std[...], tbf[:, 128 * h : 128 * h + 128], preferred_element_type=F32)
+            partial[h] = half.reshape(MARKS, 64, 128)
+        pair[h, d] = push(partial.at[h, block(d, 1 - c)], pair_in.at[h, d], prs.at[h, d], prr.at[h, d], partner)
+    for h, d in steps:
+        if d:
+            pair[h, d].wait_recv()
+            sk_out[h, d] = partial[h, block(d, c)] + pair_in[h, d]
+            along[h, d] = push(sk_out.at[h, d], sk_in.at[h, d], sks.at[h, d], skr.at[h, d], at_x(d))
+    started += list(pair.values()) + list(along.values())
+
+    def own_half(h):
+        pair[h, 0].wait_recv()
+        value = partial[h, block(0, c)] + pair_in[h, 0]
+        for d in (1, 3, 2):
+            along[h, d].wait_recv()
+            value = value + sk_in[h, d]
+        sketch[:, 128 * h : 128 * h + 128] = value
+        return value.astype(BF16)
+
+    def to_all_marks(buf, sends, recvs):
+        copies = [
+            push(buf.at[mark], buf.at[mark], sends.at[k], recvs.at[k], to)
+            for k, to in enumerate([at_other(d) for d in FAR_X] + [at_x(d) for d in FAR_X] + [partner])
+        ]
+        started.extend(copies)
+        return copies
+
+    yr0[mark] = own_half(0)
+    out = {d: push(yr0.at[mark], yr0.at[mark], yxs.at[d], yxr.at[d], at_x(d)) for d in FAR_X}
+    over = {0: push(yr0.at[mark], yr0.at[mark], yps.at[0], ypr.at[0], partner)}
+    yr1[mark] = own_half(1)
+    second_half = to_all_marks(yr1, y2s, y2r)
     for d in (1, 3, 2):
-        along[d].wait_recv()
-        own_sketch = own_sketch + sk_in[d]
-    sketch[...] = own_sketch
-    started += list(pair.values()) + list(along.values())
-
-    def gather_over_mark(buf, xs, xr, ps_, pr_):
-        out = {d: push(buf.at[mark], buf.at[mark], xs.at[d], xr.at[d], at_x(d)) for d in FAR_X}
-        over = {0: push(buf.at[mark], buf.at[mark], ps_.at[0], pr_.at[0], partner)}
-        for d in (1, 3, 2):
-            out[d].wait_recv()
-            slot = ((x + XS - d) % XS) * CORES + c
-            over[d] = push(buf.at[slot], buf.at[slot], ps_.at[d], pr_.at[d], partner)
-        for d in (0, 1, 3, 2):
-            over[d].wait_recv()
-        started.extend(list(out.values()) + list(over.values()))
-
-    yr[mark] = own_sketch.astype(BF16)
-    gather_over_mark(yr, yxs, yxr, yps, ypr)
-    rounded = yr[...].reshape(512, 256)
-
-    left = dot_cols(rounded, rounded[:, 0:128])
-    gs[0:256, :] = left
-    gs[256:384, :] = dot_cols(rounded[:, 128:256], rounded[:, 128:256])
-    part = pl.multiple_of(mark * 48, 8)
-    ga[y] = gs[pl.ds(part, 24), :]
-    gb[z] = gs[pl.ds(pl.multiple_of(part + 24, 8), 24), :]
-    first = []
+        out[d].wait_recv()
+        slot = ((x + XS - d) % XS) * CORES + c
+        over[d] = push(yr0.at[slot], yr0.at[slot], yps.at[d], ypr.at[d], partner)
+    for d in (0, 1, 3, 2):
+        over[d].wait_recv()
+    started += list(out.values()) + list(over.values())
+
+    rounded0 = yr0[...].reshape(512, 128)
+
+    def to_rings(left, right, sems, there, back):
+        (lslot, lto), (rslot, rto) = there, back
+        copies = []
+        for d in FAR_RING:
+            copies.append(push(left.at[lslot], left.at[lslot], sems[0].at[0, d - 1], sems[1].at[0, d - 1], lto(d)))
+            copies.append(push(right.at[rslot], right.at[rslot], sems[0].at[1, d - 1], sems[1].at[1, d - 1], rto(d)))
+        started.extend(copies)
+        return copies
+
+    def arrived(copies):
+        for copy in copies:
+            copy.wait_recv()
+
+    along_y, along_z = (y, at_y), (z, at_z)
+
+    g1[...] = dot_cols(rounded0, rounded0)
+    part = pl.multiple_of(mark * 16, 16)
+    ga1[y] = g1[pl.ds(part, 8), :]
+    gb1[z] = g1[pl.ds(pl.multiple_of(part + 8, 8), 8), :]
+    first1 = to_rings(ga1, gb1, (g11s, g11r), along_y, along_z)
+    arrived(second_half)
+    rounded1 = yr1[...].reshape(512, 128)
+    g2[0:128, :] = dot_cols(rounded1, rounded0)
+    g2[128:256, :] = dot_cols(rounded1, rounded1)
+    part = pl.multiple_of(mark * 32, 32)
+    ga2[y] = g2[pl.ds(part, 16), :]
+    gb2[z] = g2[pl.ds(pl.multiple_of(part + 16, 16), 16), :]
+    first2 = to_rings(ga2, gb2, (g12s, g12r), along_y, along_z)
+
+    pva[...] = dot_cols(std[...], rounded0).reshape(RING, 32, 128)
+    pm[...] = dot_cols(std[...], rounded1)
+    for q in range(RING * RING):
+        pvb[q % RING, 4 * (q // RING) : 4 * (q // RING) + 4, :] = pm[4 * q : 4 * q + 4, :]
+
+    pfirst = []
+
+    def pass_on(distances):
+        for d in distances:
+            pfirst.append(push(pva.at[(z + d) % RING], pza.at[d], z1s.at[0, d - 1], z1r.at[0, d - 1], at_z(d)))
+            pfirst.append(push(pvb.at[(y + d) % RING], pzb.at[d], z1s.at[1, d - 1], z1r.at[1, d - 1], at_y(d)))
+
+    pass_on((3, 5, 2, 6, 1, 7))
+    arrived(first1)
+    ha1[z] = jnp.sum(ga1[...], axis=0)
+    hb1[y] = jnp.sum(gb1[...], axis=0)
+    second1 = to_rings(ha1, hb1, (g21s, g21r), along_z, along_y)
+    pass_on((4,))
+    arrived(first2)
+    ha2[z] = jnp.sum(ga2[...], axis=0)
+    hb2[y] = jnp.sum(gb2[...], axis=0)
+    second2 = to_rings(ha2, hb2, (g22s, g22r), along_z, along_y)
+    arrived(second1)
+    gf1[mark] = jnp.concatenate([jnp.sum(ha1[...], axis=0), jnp.sum(hb1[...], axis=0)], axis=0)
+
+    over1 = to_all_marks(gf1, fxs, fxr)
+    arrived(second2)
+    gf2[mark] = jnp.concatenate([jnp.sum(ha2[...], axis=0), jnp.sum(hb2[...], axis=0)], axis=0)
+    under = to_all_marks(gf2, f2s, f2r)
+    arrived(over1)
+    g1[...] = gf1[...].reshape(128, 128)
+
+    psecond = []
+    arrived(pfirst)
+    started.extend(pfirst)
+    asum, bsum = pva[z], pvb[y]
+    for d in range(1, RING):
+        asum, bsum = asum + pza[d], bsum + pzb[d]
+    for q in range(RING):
+        psa[q] = asum[4 * q : 4 * q + 4, :]
+        psb[q] = bsum[4 * q : 4 * q + 4, :]
     for d in FAR_RING:
-        first.append(push(ga.at[y], ga.at[y], g1s.at[0, d - 1], g1r.at[0, d - 1], at_y(d)))
-        first.append(push(gb.at[z], gb.at[z], g1s.at[1, d - 1], g1r.at[1, d - 1], at_z(d)))
-
-    pv[...] = dot_cols(std[...], rounded).reshape(RING, 32, 256)
-
-    for copy in first:
-        copy.wait_recv()
-    ha[z] = jnp.sum(ga[...], axis=0)
-    hb[y] = jnp.sum(gb[...], axis=0)
-    second = []
-    for d in FAR_RING:
-        second.append(push(ha.at[z], ha.at[z], g2s.at[0, d - 1], g2r.at[0, d - 1], at_z(d)))
-        second.append(push(hb.at[y], hb.at[y], g2s.at[1, d - 1], g2r.at[1, d - 1], at_y(d)))
-    zsum = {}
-    for d in FAR_RING:
-        zsum[d] = push(pv.at[(z + d) % RING], pz.at[d], z1s.at[d], z1r.at[d], at_z(d))
-    for copy in second:
-        copy.wait_recv()
-    started += first + second
-    gf[mark] = jnp.concatenate([jnp.sum(ha[...], axis=0), jnp.sum(hb[...], axis=0)], axis=0)
-    gather_over_mark(gf, fxs, fxr, fps, fpr)
-    gs[...] = gf[...].reshape(384, 128)
-
-    psum = pv[z]
-    for d in range(1, RING):
-        zsum[d].wait_recv()
-        psum = psum + pz[d]
-    for q in range(RING):
-        ps[q] = psum[4 * q : 4 * q + 4, :]
-    ysum = {d: push(ps.at[(y + d) % RING], py.at[d], y1s.at[d], y1r.at[d], at_y(d)) for d in FAR_RING}
-    started += list(zsum.values()) + list(ysum.values())
-
-    one = inverse_factor([gs[8 * g : 8 * g + 8, :] for g in range(16)])
+        psecond.append(push(psa.at[(y + d) % RING], pya.at[d], y1s.at[0, d - 1], y1r.at[0, d - 1], at_y(d)))
+        psecond.append(push(psb.at[(z + d) % RING], pyb.at[d], y1s.at[1, d - 1], y1r.at[1, d - 1], at_z(d)))
+    started.extend(psecond)
+
+    one = inverse_factor([g1[8 * g : 8 * g + 8, :] for g in range(16)])
     for g in range(16):
         inv[0, 8 * g : 8 * g + 8, :] = one[g]
+    arrived(under)
+    g2[...] = gf2[...].reshape(256, 128)
     inv1 = inv[0]
-    low = dot_t(gs[128:256, :], inv1)
-    gs[256:384, :] = gs[256:384, :] - dot_t(low, low)
-
+    low = dot_t(g2[0:128, :], inv1)
+    g2[128:256, :] = g2[128:256, :] - dot_t(low, low)
     head = dot_t(sketch[:, 0:128], inv1)
     middle = sketch[:, 128:256] - dot_t(head, low)
 
-    two = inverse_factor([gs[256 + 8 * g : 264 + 8 * g, :] for g in range(16)])
+    def finish_projection():
+        arrived(psecond)
+        left, right = psa[y], psb[z]
+        for d in range(1, RING):
+            left, right = left + pya[d], right + pyb[d]
+        left = jnp.concatenate([left, left], axis=0)
+        right = jnp.concatenate([right, right], axis=0)
+        head_p = dot_t(left, inv1)
+        loadings_ref[:, 0:128] = head_p[0:4]
+        middles.append(right - dot_t(head_p, low))
+
+    middles = [middle]
+    two = inverse_factor([g2[128 + 8 * g : 136 + 8 * g, :] for g in range(16)], {10: finish_projection})
     for g in range(16):
         inv[1, 8 * g : 8 * g + 8, :] = two[g]
     inv2 = inv[1]
-    projected = ps[y]
-    for d in range(1, RING):
-        ysum[d].wait_recv()
-        projected = projected + py[d]
-    projected = jnp.concatenate([projected, projected], axis=0)
-    head_p = dot_t(projected[:, 0:128], inv1)
-    middle_p = projected[:, 128:256] - dot_t(head_p, low)
-    tail = dot_t(jnp.concatenate([middle, middle_p], axis=0), inv2)
+    tail = dot_t(jnp.concatenate(middles, axis=0), inv2)
     basis_ref[:, 0:128] = math.sqrt(total) * head
     basis_ref[:, 128:256] = math.sqrt(total) * tail[0:64]
-    loadings_ref[:, 0:128] = head_p[0:4]
     loadings_ref[:, 128:256] = tail[64:68]
 
     for copy in started:
@@ -318,29 +377,30 @@
             pltpu.VMEM((RING, RING, 4, 128), BF16),
             pltpu.VMEM((256, 256), F32),
             pltpu.VMEM((256, 256), BF16),
-            pltpu.VMEM((XS, 64, 256), F32),
-            pltpu.VMEM((XS, 64, 256), F32),
-            pltpu.VMEM((XS, 64, 256), F32),
-            pltpu.VMEM((XS, 64, 256), F32),
+            pltpu.VMEM((2, MARKS, 64, 128), F32),
+            pltpu.VMEM((2, XS, 64, 128), F32),
+            pltpu.VMEM((2, XS, 64, 128), F32),
+            pltpu.VMEM((2, XS, 64, 128), F32),
             pltpu.VMEM((64, 256), F32),
-            pltpu.VMEM((MARKS, 64, 256), BF16),
-            pltpu.VMEM((384, 128), F32),
-            pltpu.VMEM((RING, 24, 128), F32),
-            pltpu.VMEM((RING, 24, 128), F32),
-            pltpu.VMEM((RING, 24, 128), F32),
-            pltpu.VMEM((RING, 24, 128), F32),
-            pltpu.VMEM((MARKS, 48, 128), F32),
+            *[pltpu.VMEM((MARKS, 64, 128), BF16)] * 2,
+            pltpu.VMEM((128, 128), F32),
+            pltpu.VMEM((256, 128), F32),
+            *[pltpu.VMEM((RING, 8, 128), F32)] * 4,
+            pltpu.VMEM((MARKS, 16, 128), F32),
+            *[pltpu.VMEM((RING, 16, 128), F32)] * 4,
+            pltpu.VMEM((MARKS, 32, 128), F32),
             pltpu.VMEM((2, 128, 128), F32),
-            pltpu.VMEM((RING, 32, 256), F32),
-            pltpu.VMEM((RING, 32, 256), F32),
-            pltpu.VMEM((RING, 4, 256), F32),
-            pltpu.VMEM((RING, 4, 256), F32),
+            *[pltpu.VMEM((RING, 32, 128), F32)] * 4,
+            *[pltpu.VMEM((RING, 4, 128), F32)] * 4,
+            pltpu.VMEM((256, 128), F32),
             dma((6,)),
             *two_rings, *two_rings,
-            *[dma((XS,))] * 8,
+            *[dma((2, XS))] * 4,
+            *[dma((XS,))] * 4,
+            *[dma((MARKS - 1,))] * 2,
+            *two_rings, *two_rings, *two_rings, *two_rings,
+            *[dma((MARKS - 1,))] * 4,
             *two_rings, *two_rings,
-            *[dma((XS,))] * 4,
-            *[dma((RING,))] * 4,
         ],
         compiler_params=pltpu.CompilerParams(
             collective_id=0, has_side_effects=True, vmem_limit_bytes=24 * 1024 * 1024

time: 62.8 us -> 58.6 us (0.933)
  Pallas kernels: 62 us -> 57.8 us
    pallas_call x1, Pallas kernels: 61.4 us -> 57.1 us  [per_device(): pl.pallas_call(functools.partial(kernel, total), out_shape=tuple((pltpu.V...]
where the time goes in v3:
time: 58.6 us; the launch traced here: 58.4 us
  Pallas kernels  57.8 us (99%)
  between operations  0.64 us (1%)
    pallas_call x1, Pallas kernels, per_device(): pl.pallas_call(functools.partial(kernel, total), out_shape=tuple((pltpu.V...  57.1 us

profile of v3, /device:TPU:1, one launch (start us, length us, event | category | flops | bytes accessed | tf_op | source)
XLA Modules:
  0.0 58.4 jit_solution(1263197721998222216)
XLA Ops:
  0.6 57.1 %shard_map.68 = (f32[64,256]{1,0:T(8,128)S(1)}, f32[4,256]{1,0:T(4,128)S(1)}) custom-call(bf16[512,256]{1,0:T(8,128)(2,1)} %dosage_hbm.1, s32[2,128]{1,0:T(2,128)} %bitcast.4, s32[2,128]{1,0:T(2,128)} %bitcast.5, f32[4,128]{1,0:T(4,128)} %bitcast.3, bf16[4,256]{1,0:T(4,128)(2,1)} %test_hbm.1), custom_call_target="tpu_custom_call" | custom-call | tf_op jit(solution)/shard_map/pallas_call | solution.py:365
  57.8 0.7 %shard_map.69 = (f32[64,256]{1,0:T(8,128)}, f32[4,256]{1,0:T(4,128)}) custom-call(f32[64,256]{1,0:T(8,128)S(1)} %get-tuple-element.4.basis_in, f32[4,256]{1,0:T(4,128)S(1)} %get-tuple-element.5.loadings_in), custom_call_target="tpu_custom_call" | custom-call | tf_op jit(solution)/shard_map/pallas_call | solution.py:409

commit v4 on v3

--- a/solution.py
+++ b/solution.py
@@ -19,6 +19,11 @@
 HIGHEST = lax.Precision.HIGHEST
 
 
+def lanes_of(value, k):
+    lane = lax.broadcasted_iota(jnp.int32, (8, 128), 1)
+    return jnp.broadcast_to(jnp.sum(jnp.where(lane == k, value, 0.0), axis=1, keepdims=True), (8, 128))
+
+
 def spread(column):
     return jnp.broadcast_to(column, (8, 128))
 
@@ -28,48 +33,46 @@
     row = lax.broadcasted_iota(jnp.int32, (8, 128), 0)
     rows = list(groups)
     count = len(rows)
-    own = [spread(rows[0][:, j : j + 1]) for j in range(8)]
+    own = [lanes_of(rows[0], j) for j in range(8)]
     for b in range(count):
         if meanwhile is not None and b in meanwhile:
             meanwhile[b]()
         start = 8 * b
         inside = (lane >= start) & (lane < start + 8)
-        cols = {g: [spread(rows[g][:, start + j : start + j + 1]) for j in range(8)] for g in range(b + 1, count)}
+        cols = {g: [] for g in range(b + 1, count)}
+        for j in range(8):
+            for g in range(b + 1, count):
+                cols[g].append(lanes_of(rows[g], start + j))
         last = b + 1 == count
-        following = None if last else [spread(rows[b + 1][:, start + 8 + j : start + 9 + j]) for j in range(8)]
+        following = None if last else [lanes_of(rows[b + 1], start + 8 + j) for j in range(8)]
+        theirs = None if last else list(cols[b + 1])
         panel = jnp.where(inside, jnp.where(lane - start == row, 1.0, 0.0), rows[b])
-        scaled, roots, upper, near = [], [], {}, []
+        done = panel
         for k in range(8):
-            root = lax.rsqrt(spread(own[k][k : k + 1]))
-            line = spread(panel[k : k + 1]) * root
-            below = own[k] * root
+            pivot = spread(own[k][k : k + 1])
+            whole = 1.0 / pivot
+            line = spread(panel[k : k + 1])
+            done = jnp.where(row == k, line * lax.rsqrt(pivot), done)
+            normed = line * whole
+            panel = jnp.where(row == k, normed, panel - own[k] * normed)
+            across = {j: spread(own[j][k : k + 1]) * whole for j in range(k + 1, 8)}
             for j in range(k + 1, 8):
-                upper[k, j] = spread(own[j][k : k + 1]) * root
-                own[j] = own[j] - below * upper[k, j]
-            panel = jnp.where(row == k, line, panel - jnp.where(row > k, below, 0.0) * line)
-            scaled.append(line)
-            roots.append(root)
+                own[j] = jnp.where(row == k, across[j], own[j] - own[k] * across[j])
             if not last:
-                theirs = cols[b + 1]
-                factor = theirs[k] * root
+                factor = theirs[k]
                 for j in range(k + 1, 8):
-                    theirs[j] = theirs[j] - factor * upper[k, j]
+                    theirs[j] = theirs[j] - factor * across[j]
+                scaled = factor * whole
                 for j in range(8):
-                    following[j] = following[j] - factor * spread(factor[j : j + 1])
-                near.append(factor)
-        rows[b] = panel
+                    following[j] = following[j] - factor * spread(scaled[j : j + 1])
+        rows[b] = done
+        lines = [spread(panel[k : k + 1]) for k in range(8)]
         for g in range(b + 1, count):
             left = jnp.where(inside, 0.0, rows[g])
-            theirs = cols[g]
-            for k in range(8):
-                if g == b + 1:
-                    factor = near[k]
-                else:
-                    factor = theirs[k] * roots[k]
-                    for j in range(k + 1, 8):
-                        theirs[j] = theirs[j] - factor * upper[k, j]
-                left = left - factor * scaled[k]
-            rows[g] = left
+            terms = [cols[g][k] * lines[k] for k in range(8)]
+            while len(terms) > 1:
+                terms = [terms[i] + terms[i + 1] for i in range(0, len(terms), 2)]
+            rows[g] = left - terms[0]
         own = following
     return [jnp.where(lane <= row + 8 * g, rows[g], 0.0) for g in range(count)]
 
@@ -87,7 +90,7 @@
     dosage_hbm, alt_hbm, obs_hbm, weight_hbm, test_hbm,
     basis_ref, loadings_ref,
     dosage, alt, obs, weight, std, ta, tb, tfull, tbf,
-    partial, pair_in, sk_out, sk_in, sketch, yr0, yr1,
+    theirs, mine, pair_in, sk_out, sk_in, sketch, yr0, yr1,
     g1, g2, ga1, gb1, ha1, hb1, gf1, ga2, gb2, ha2, hb2, gf2, inv,
     pva, pvb, pza, pzb, psa, psb, pya, pyb, pm,
     in_sem,
@@ -180,23 +183,31 @@
     def block(d, core):
         return ((x + d) % XS) * CORES + core
 
+    def products(core, h):
+        blocks = [std[pl.ds(pl.multiple_of(block(d, core) * 64, 64), 64), :] for d in (2, 1, 3, 0)]
+        return jnp.dot(
+            jnp.concatenate(blocks, axis=0), tbf[:, 128 * h : 128 * h + 128], preferred_element_type=F32
+        )
+
     steps = [(h, d) for h in range(2) for d in (2, 1, 3, 0)]
+    place = {2: 0, 1: 1, 3: 2, 0: 3}
     pair, along = {}, {}
-    for h, d in steps:
-        if d == 2:
-            half = jnp.dot(std[...], tbf[:, 128 * h : 128 * h + 128], preferred_element_type=F32)
-            partial[h] = half.reshape(MARKS, 64, 128)
-        pair[h, d] = push(partial.at[h, block(d, 1 - c)], pair_in.at[h, d], prs.at[h, d], prr.at[h, d], partner)
+    for h in range(2):
+        theirs[h] = products(1 - c, h).reshape(XS, 64, 128)
+        for d in (2, 1, 3, 0):
+            pair[h, d] = push(theirs.at[h, place[d]], pair_in.at[h, d], prs.at[h, d], prr.at[h, d], partner)
+    for h in range(2):
+        mine[h] = products(c, h).reshape(XS, 64, 128)
     for h, d in steps:
         if d:
             pair[h, d].wait_recv()
-            sk_out[h, d] = partial[h, block(d, c)] + pair_in[h, d]
+            sk_out[h, d] = mine[h, place[d]] + pair_in[h, d]
             along[h, d] = push(sk_out.at[h, d], sk_in.at[h, d], sks.at[h, d], skr.at[h, d], at_x(d))
     started += list(pair.values()) + list(along.values())
 
     def own_half(h):
         pair[h, 0].wait_recv()
-        value = partial[h, block(0, c)] + pair_in[h, 0]
+        value = mine[h, place[0]] + pair_in[h, 0]
         for d in (1, 3, 2):
             along[h, d].wait_recv()
             value = value + sk_in[h, d]
@@ -284,6 +295,9 @@
     arrived(second2)
     gf2[mark] = jnp.concatenate([jnp.sum(ha2[...], axis=0), jnp.sum(hb2[...], axis=0)], axis=0)
     under = to_all_marks(gf2, f2s, f2r)
+    drained = len(started)
+    for copy in started[: drained - 2 * (MARKS - 1)]:
+        copy.wait_send()
     arrived(over1)
     g1[...] = gf1[...].reshape(128, 128)
 
@@ -333,7 +347,7 @@
     basis_ref[:, 128:256] = math.sqrt(total) * tail[0:64]
     loadings_ref[:, 128:256] = tail[64:68]
 
-    for copy in started:
+    for copy in started[drained - 2 * (MARKS - 1) :]:
         copy.wait_send()
 
 
@@ -377,7 +391,7 @@
             pltpu.VMEM((RING, RING, 4, 128), BF16),
             pltpu.VMEM((256, 256), F32),
             pltpu.VMEM((256, 256), BF16),
-            pltpu.VMEM((2, MARKS, 64, 128), F32),
+            *[pltpu.VMEM((2, XS, 64, 128), F32)] * 2,
             pltpu.VMEM((2, XS, 64, 128), F32),
             pltpu.VMEM((2, XS, 64, 128), F32),
             pltpu.VMEM((2, XS, 64, 128), F32),

time: 58.6 us -> 57.7 us (0.985)
  Pallas kernels: 57.8 us -> 56.9 us
    pallas_call x1, Pallas kernels: 57.1 us -> 56.3 us  [per_device(): pl.pallas_call(functools.partial(kernel, total), out_shape=tuple((pltpu.V...]
where the time goes in v4:
time: 57.7 us; the launch traced here: 57.6 us
  Pallas kernels  56.9 us (99%)
  between operations  0.64 us (1%)
    pallas_call x1, Pallas kernels, per_device(): pl.pallas_call(functools.partial(kernel, total), out_shape=tuple((pltpu.V...  56.3 us

profile of v4, /device:TPU:1, one launch (start us, length us, event | category | flops | bytes accessed | tf_op | source)
XLA Modules:
  0.0 57.6 jit_solution(14475785855458714914)
XLA Ops:
  0.6 56.3 %shard_map.68 = (f32[64,256]{1,0:T(8,128)S(1)}, f32[4,256]{1,0:T(4,128)S(1)}) custom-call(bf16[512,256]{1,0:T(8,128)(2,1)} %dosage_hbm.1, s32[2,128]{1,0:T(2,128)} %bitcast.4, s32[2,128]{1,0:T(2,128)} %bitcast.5, f32[4,128]{1,0:T(4,128)} %bitcast.3, bf16[4,256]{1,0:T(4,128)(2,1)} %test_hbm.1), custom_call_target="tpu_custom_call" | custom-call | tf_op jit(solution)/shard_map/pallas_call | solution.py:379
  56.9 0.7 %shard_map.69 = (f32[64,256]{1,0:T(8,128)}, f32[4,256]{1,0:T(4,128)}) custom-call(f32[64,256]{1,0:T(8,128)S(1)} %get-tuple-element.4.basis_in, f32[4,256]{1,0:T(4,128)S(1)} %get-tuple-element.5.loadings_in), custom_call_target="tpu_custom_call" | custom-call | tf_op jit(solution)/shard_map/pallas_call | solution.py:423
